TPU v7x, 32 devices: a whole 2x2x4 slice. The times are simulated.
32 devices in a mesh: dp: 8 (over z, x), tensor: 4 (over y, core).
Axes of the slice: x: 2, y: 2, z: 4, core: 2. Of those that a mesh axis runs over, the one named last changes fastest.
Arguments:
- ranges: bfloat16 [10240, 2652], P('dp'), may hold values from 0.049804688 to 2
- pot: float32 [10240], P('dp'), may hold values from 0.1 to 1
- w_ranges: bfloat16 [2652, 2048], P(None, 'tensor'), may hold values from -0.125 to 0.125
- w_pot: float32 [2048], P('tensor'), may hold values from -5 to 5
- bias_one: float32 [2048], P('tensor'), may hold values from -1.5 to 1.5
- w_two: bfloat16 [2048, 2048], P('dp', 'tensor'), may hold values from -0.125 to 0.125
- bias_two: float32 [2048], P('tensor'), may hold values from -1.5 to 1.5
- w_three: bfloat16 [2048, 2048], P('dp', 'tensor'), may hold values from -0.125 to 0.125
- bias_three: float32 [2048], P('tensor'), may hold values from -1.5 to 1.5
- w_out: bfloat16 [2048, 2652], P(('dp', 'tensor')), may hold values from -0.1875 to 0.1875
- bias_out: float32 [2652], replicated, may hold values from -1.5 to 1.5
Outputs:
- hand_values: float32 [10240, 2652], P(('dp', 'tensor'))
All inputs are finite; a program needn't handle non-finite values.
Results may differ from a plain program's by a relative error of at most 0.0039.
Values may be sent and summed in bfloat16 or wider, within the bound.
A program may use at most 128 MiB of HBM per device.

v0:
```python
import jax
import jax.numpy as jnp
from jax import lax
from jax.sharding import PartitionSpec as P


def relu_round(pre):
    return jnp.maximum(pre, 0.0).astype(jnp.bfloat16)


def fold_rows(left, piece):
    return jnp.dot(left, piece, preferred_element_type=jnp.float32)


def local(
    ranges, pot, w_ranges, w_pot, bias_one, w_two, bias_two, w_three, bias_three, w_out, bias_out
):
    groups = lax.axis_size("tensor")
    position = lax.axis_index("tensor")
    states = ranges.shape[0]
    own_count = states // groups
    lowest = position * own_count
    own_ranges = lax.dynamic_slice_in_dim(ranges, lowest, own_count, 0)
    pre = jnp.dot(ranges, w_ranges, preferred_element_type=jnp.float32)
    hidden = relu_round(pre + pot[:, None] * w_pot[None, :] + bias_one[None, :])
    for weight, bias in ((w_two, bias_two), (w_three, bias_three)):
        whole = lax.all_gather(hidden, "tensor", axis=1, tiled=True)
        summed = fold_rows(whole, lax.all_gather(weight, "dp", axis=0, tiled=True))
        hidden = relu_round(summed + bias[None, :])
    own_hidden = lax.all_to_all(hidden, "tensor", split_axis=0, concat_axis=1, tiled=True)
    out_block = lax.all_gather(w_out, "tensor", axis=0, tiled=True)
    values = (
        fold_rows(own_hidden, lax.all_gather(out_block, "dp", axis=0, tiled=True))
        + bias_out[None, :]
    )
    weights = own_ranges.astype(jnp.float32)
    error = jnp.sum(weights * values, axis=1) / jnp.sum(weights, axis=1)
    return values - error[:, None]


def solution(mesh):
    in_specs = (
        P("dp", None),
        P("dp"),
        P(None, "tensor"),
        P("tensor"),
        P("tensor"),
        P("dp", "tensor"),
        P("tensor"),
        P("dp", "tensor"),
        P("tensor"),
        P(("dp", "tensor"), None),
        P(),
    )
    out_specs = P(("dp", "tensor"), None)
    return jax.shard_map(local, mesh=mesh, in_specs=in_specs, out_specs=out_specs, check_vma=False)
```

profile of v0, /device:TPU:0, one launch (start us, length us, event | category | flops | bytes accessed | tf_op | source)
XLA Modules:
  0.0 390.5 jit_solution(3218508177793755378)
XLA Ops:
  6.5 0.0 copy-start
  6.5 0.0 all-gather.9.cloned.1.call-start
  6.5 0.7 all-gather.9.cloned.1.call-update
  7.3 0.0 copy-start.2
  7.3 0.0 all-gather.7.cloned.1.call-start
  7.3 1.0 copy-done
  8.3 8.0 %fusion.5 = bf16[1280,512]{1,0:T(8,128)(2,1)} fusion(bf16[1280,2652]{0,1:T(8,128)(2,1)} %param.11, bf16[2652,512]{1,0:T(8,128)(2,1)S(1)} %copy-done, f32[512]{0:T(512)} %param.15, f32[512]{0:T(512)} %param.14, f32[1280]{0:T(1024)} %param.12), kind=kOutput, calls=%fused_computation.11 | convolution fusion | flops 3479306240 | bytes 10824704 | tf_op jit(solution)/shard_map/dot_general | solution.py:24
  16.3 0.0 all-gather.7.cloned.1.call-update
  16.4 0.0 all-gather.15.cloned.1.call-start
  16.4 0.7 all-gather.15.cloned.1.call-update
  17.1 0.0 all-gather.13.cloned.1.call-start
  17.2 0.5 all-gather.13.cloned.1.call-update
  17.7 0.0 all-gather.11.cloned.1.call-start
  17.7 43.6 %all-gather.9.cloned.1.call-done = bf16[2048,512]{1,0:T(8,128)(2,1)} async-done(((bf16[256,512]{1,0:T(8,128)(2,1)}), bf16[2048,512]{1,0:T(8,128)(2,1)}) %all-gather.9.cloned.1.call-update) | async-done | bytes 2097168 | tf_op jit(solution)/shard_map/all_gather | solution.py:28
  61.3 40.5 %all-gather.7.cloned.1.call-done = bf16[1280,2048]{1,0:T(8,128)(2,1)} async-done(((bf16[1280,512]{1,0:T(8,128)(2,1)}), bf16[1280,2048]{1,0:T(8,128)(2,1)}) %all-gather.7.cloned.1.call-update) | async-done | bytes 5242896 | tf_op jit(solution)/shard_map/all_gather | solution.py:27
  101.8 0.0 copy-done.2
  101.8 7.1 %fusion.6 = bf16[1280,512]{1,0:T(8,128)(2,1)} fusion(bf16[1280,2048]{1,0:T(8,128)(2,1)} %all-gather.7.cloned.1.call-done, bf16[2048,512]{1,0:T(8,128)(2,1)} %all-gather.9.cloned.1.call-done, f32[512]{0:T(512)S(1)} %copy-done.2), kind=kOutput, calls=%fused_computation.12 | convolution fusion | flops 2686320640 | bytes 8652800 | tf_op jit(solution)/shard_map/dot_general | solution.py:12
  108.9 0.0 copy-start.3
  108.9 0.0 all-gather.11.cloned.1.call-update
  109.0 0.0 all-gather.17.cloned.1.call-start
  109.0 12.9 %all-gather.15.cloned.1.call-done = bf16[256,2652]{1,0:T(8,128)(2,1)} async-done(((bf16[64,2652]{1,0:T(8,128)(2,1)}), bf16[256,2652]{1,0:T(8,128)(2,1)}) %all-gather.15.cloned.1.call-update) | async-done | bytes 1357840 | tf_op jit(solution)/shard_map/all_gather | solution.py:31
  122.0 0.0 all-gather.17.cloned.1.call-update
  122.0 51.1 %all-gather.13.cloned.1.call-done = bf16[2048,512]{1,0:T(8,128)(2,1)} async-done(((bf16[256,512]{1,0:T(8,128)(2,1)}), bf16[2048,512]{1,0:T(8,128)(2,1)}) %all-gather.13.cloned.1.call-update) | async-done | bytes 2097168 | tf_op jit(solution)/shard_map/all_gather | solution.py:28
  173.1 40.4 %all-gather.11.cloned.1.call-done = bf16[1280,2048]{1,0:T(8,128)(2,1)} async-done(((bf16[1280,512]{1,0:T(8,128)(2,1)}), bf16[1280,2048]{1,0:T(8,128)(2,1)}) %all-gather.11.cloned.1.call-update) | async-done | bytes 5242896 | tf_op jit(solution)/shard_map/all_gather | solution.py:27
  213.5 0.0 copy-done.3
  213.5 7.1 %fusion.7 = bf16[1280,512]{1,0:T(8,128)(2,1)} fusion(bf16[1280,2048]{1,0:T(8,128)(2,1)} %all-gather.11.cloned.1.call-done, bf16[2048,512]{1,0:T(8,128)(2,1)} %all-gather.13.cloned.1.call-done, f32[512]{0:T(512)S(1)} %copy-done.3), kind=kOutput, calls=%fused_computation.13 | convolution fusion | flops 2686320640 | bytes 8652800 | tf_op jit(solution)/shard_map/dot_general | solution.py:12
  220.6 4.6 %all-to-all-start = ((bf16[4,320,512]{2,1,0:T(8,128)(2,1)}), bf16[4,320,512]{2,1,0:T(8,128)(2,1)}, u32[]{:S(2)}, u32[]{:S(2)}) async-start(bf16[4,320,512]{2,1,0:T(8,128)(2,1)} %bitcast.12), calls=%async_computation | async-start | bytes 2621440 | tf_op jit(solution)/shard_map/all_to_all | solution.py:30
  225.1 4.6 %constant_dynamic-slice_fusion = bf16[320,2652]{0,1:T(8,128)(2,1)} fusion(bf16[1280,2652]{0,1:T(8,128)(2,1)} %param.11, s32[]{:T(128)S(6)} %select_n.3), kind=kLoop, calls=%fused_computation.15 | loop fusion | bytes 3394564 | tf_op jit(solution)/shard_map/dynamic_slice | solution.py:23
  229.7 0.0 copy-start.1
  229.7 4.0 %copy.17 = bf16[320,2652]{1,0:T(8,128)(2,1)} copy(bf16[320,2652]{0,1:T(8,128)(2,1)} %constant_dynamic-slice_fusion) | data formatting | bytes 3394560
  233.7 8.6 %all-to-all-done = bf16[4,320,512]{2,1,0:T(8,128)(2,1)} async-done(((bf16[4,320,512]{2,1,0:T(8,128)(2,1)}), bf16[4,320,512]{2,1,0:T(8,128)(2,1)}, u32[]{:S(2)}, u32[]{:S(2)}) %all-to-all-start) | async-done | bytes 1310752 | tf_op jit(solution)/shard_map/all_to_all | solution.py:30
  242.2 2.6 copy.18
  244.8 127.6 %all-gather.17.cloned.1.call-done = bf16[2048,2652]{1,0:T(8,128)(2,1)} async-done(((bf16[256,2652]{1,0:T(8,128)(2,1)}), bf16[2048,2652]{1,0:T(8,128)(2,1)}) %all-gather.17.cloned.1.call-update) | async-done | bytes 10862608 | tf_op jit(solution)/shard_map/all_gather | solution.py:33
  372.4 0.0 copy-done.1
  372.4 9.1 %convert_reduce_fusion = (f32[320]{0:T(512)S(1)}, f32[320]{0:T(512)S(1)}, f32[320,2652]{1,0:T(8,128)S(1)}) fusion(bf16[320,2652]{1,0:T(8,128)(2,1)} %copy.17, f32[2652]{0:T(1024)S(1)} %copy-done.1, bf16[320,2048]{1,0:T(8,128)(2,1)} %bitcast.13, bf16[2048,2652]{1,0:T(8,128)(2,1)} %all-gather.17.cloned.1.call-done), kind=kOutput, calls=%fused_computation | convolution fusion | flops 3480272128 | bytes 17278320 | tf_op jit(solution)/shard_map/dot_general | solution.py:12
  381.6 2.1 broadcast_subtract_fusion
  (1 shorter events, 0.0 us)
Async XLA Ops:
  6.5 1.8 copy-start
  6.5 54.8 %all-gather.9.cloned.1.call-start = ((), (), s32[]{:S(2)}) async-start(), calls=%async_computation.2 | async-start | bytes 2359296 | tf_op jit(solution)/shard_map/all_gather | solution.py:28
  7.3 94.6 %copy-start.2 = (f32[512]{0:T(512)S(1)}, f32[512]{0:T(512)}, u32[]{:S(2)}) copy-start(f32[512]{0:T(512)} %param.17) | copy-start | bytes 6148
  7.3 94.6 %all-gather.7.cloned.1.call-start = ((), (), s32[]{:S(2)}) async-start(), calls=%async_computation.1 | async-start | bytes 6553600 | tf_op jit(solution)/shard_map/all_gather | solution.py:27
  16.4 105.6 %all-gather.15.cloned.1.call-start = ((), (), s32[]{:S(2)}) async-start(), calls=%async_computation.5 | async-start | bytes 1720320 | tf_op jit(solution)/shard_map/all_gather | solution.py:31
  17.1 156.0 %all-gather.13.cloned.1.call-start = ((), (), s32[]{:S(2)}) async-start(), calls=%async_computation.4 | async-start | bytes 2359296 | tf_op jit(solution)/shard_map/all_gather | solution.py:28
  17.7 195.8 %all-gather.11.cloned.1.call-start = ((), (), s32[]{:S(2)}) async-start(), calls=%async_computation.3 | async-start | bytes 6553600 | tf_op jit(solution)/shard_map/all_gather | solution.py:27
  108.9 104.5 %copy-start.3 = (f32[512]{0:T(512)S(1)}, f32[512]{0:T(512)}, u32[]{:S(2)}) copy-start(f32[512]{0:T(512)} %param.19) | copy-start | bytes 6148
  109.0 263.5 %all-gather.17.cloned.1.call-start = ((), (), s32[]{:S(2)}) async-start(), calls=%async_computation.6 | async-start | bytes 12386304 | tf_op jit(solution)/shard_map/all_gather | solution.py:33
  220.6 21.7 %all-to-all-start = ((bf16[4,320,512]{2,1,0:T(8,128)(2,1)}), bf16[4,320,512]{2,1,0:T(8,128)(2,1)}, u32[]{:S(2)}, u32[]{:S(2)}) async-start(bf16[4,320,512]{2,1,0:T(8,128)(2,1)} %bitcast.12), calls=%async_computation | async-start | bytes 2621440 | tf_op jit(solution)/shard_map/all_to_all | solution.py:30
  229.7 142.7 %copy-start.1 = (f32[2652]{0:T(1024)S(1)}, f32[2652]{0:T(1024)}, u32[]{:S(2)}) copy-start(f32[2652]{0:T(1024)} %param.21) | copy-start | bytes 31828
Sparse Core Ops, SparseCore 0:
  9.5 51.7 all-gather.8
  62.9 38.9 all-gather.6
  103.4 18.5 all-gather.14
  124.0 49.0 all-gather.12
  174.5 38.9 all-gather.10
  215.5 156.8 all-gather.16
where the time goes:
time: 391 us; the launch traced here: 390 us
  waiting for transfers between devices  327 us (84%)
  matrix products  31.4 us (8%)
  between operations  13.5 us (3%)
  local copies, waits for them, and re-layouts  12.1 us (3%)
  starting transfers between devices  4.76 us (1%)
    all_gather x1, waiting for transfers between devices, local(): lax.all_gather(out_block, 'dp', axis=0, tiled=True)  128 us
    all_gather x2, waiting for transfers between devices, local(): summed = fold_rows(whole, lax.all_gather(weight, 'dp', axis=0, tiled=True))  94.6 us
    all_gather x2, waiting for transfers between devices, local(): whole = lax.all_gather(hidden, 'tensor', axis=1, tiled=True)  80.9 us
    dot_general x3, matrix products, fold_rows(): return jnp.dot(left, piece, preferred_element_type=jnp.float32)  23.3 us
    all_gather x1, waiting for transfers between devices, local(): out_block = lax.all_gather(w_out, 'tensor', axis=0, tiled=True)  12.9 us
    all_to_all x1, waiting for transfers between devices, local(): lax.all_to_all(hidden, 'tensor', split_axis=0, concat_axis=1, tiled=True)  8.56 us
    dot_general x1, matrix products, local(): pre = jnp.dot(ranges, w_ranges, preferred_element_type=jnp.float32)  8.04 us
  transfers between devices with their start and end apart: 7, of which 7 were waited for; matrix products, arithmetic and copies ran while one was open for 9% of the time, Pallas kernels for 0%

commit v1 on v0

--- a/solution.py
+++ b/solution.py
@@ -24,7 +24,16 @@
     pre = jnp.dot(ranges, w_ranges, preferred_element_type=jnp.float32)
     hidden = relu_round(pre + pot[:, None] * w_pot[None, :] + bias_one[None, :])
     for weight, bias in ((w_two, bias_two), (w_three, bias_three)):
-        whole = lax.all_gather(hidden, "tensor", axis=1, tiled=True)
+        ring = [hidden]
+        for hop in range(3):
+            ring.append(
+                lax.ppermute(ring[-1], "tensor", [(dev, (dev + 1) % 4) for dev in range(4)])
+            )
+        whole = jnp.roll(
+            jnp.concatenate(ring[::-1], axis=1),
+            (lax.axis_index("tensor") + 1) * ring[0].shape[1],
+            axis=1,
+        )
         summed = fold_rows(whole, lax.all_gather(weight, "dp", axis=0, tiled=True))
         hidden = relu_round(summed + bias[None, :])
     own_hidden = lax.all_to_all(hidden, "tensor", split_axis=0, concat_axis=1, tiled=True)

time: 391 us -> 307 us (0.79)
  waiting for transfers between devices: 327 us -> 227 us
  matrix products: 31.4 us -> 42 us
  local copies, waits for them, and re-layouts: 12.1 us -> 17.8 us
    ppermute x0 -> x6, waiting for transfers between devices: none -> 94.9 us  [local(): lax.ppermute(ring[-1], 'tensor', [(dev, (dev + 1) % 4) for dev in range(4)])]
    all_gather x2, waiting for transfers between devices: 94.6 us -> 7.91 us  [local(): summed = fold_rows(whole, lax.all_gather(weight, 'dp', axis=0, tiled=True))]
    all_gather x2 -> x0, waiting for transfers between devices: 80.9 us -> none  [local(): whole = lax.all_gather(hidden, 'tensor', axis=1, tiled=True)]
    all_gather x1, waiting for transfers between devices: 128 us -> 91.3 us  [local(): lax.all_gather(out_block, 'dp', axis=0, tiled=True)]
    dot_general x3, matrix products: 23.3 us -> 35 us  [fold_rows(): return jnp.dot(left, piece, preferred_element_type=jnp.float32)]
    all_gather x1, waiting for transfers between devices: 12.9 us -> 21.4 us  [local(): out_block = lax.all_gather(w_out, 'tensor', axis=0, tiled=True)]
    unnamed x9 -> x17, local copies, waits for them, and re-layouts: 5 us -> 8.19 us
  transfers between devices with their start and end apart: 7 -> 11, of which waited for: 7 -> 10; matrix products, arithmetic and copies ran while one was open for 9% -> 15% of each run, Pallas kernels for 0% -> 0%
where the time goes in v1:
time: 307 us; the launch traced here: 306 us
  waiting for transfers between devices  227 us (74%)
  matrix products  42 us (14%)
  local copies, waits for them, and re-layouts  17.8 us (6%)
  between operations  13.2 us (4%)
  starting transfers between devices  4.67 us (2%)
    ppermute x6, waiting for transfers between devices, local(): lax.ppermute(ring[-1], 'tensor', [(dev, (dev + 1) % 4) for dev in range(4)])  94.9 us
    all_gather x1, waiting for transfers between devices, local(): lax.all_gather(out_block, 'dp', axis=0, tiled=True)  91.3 us
    dot_general x3, matrix products, fold_rows(): return jnp.dot(left, piece, preferred_element_type=jnp.float32)  35 us
    all_gather x1, waiting for transfers between devices, local(): out_block = lax.all_gather(w_out, 'tensor', axis=0, tiled=True)  21.4 us
    all_to_all x1, waiting for transfers between devices, local(): lax.all_to_all(hidden, 'tensor', split_axis=0, concat_axis=1, tiled=True)  9.15 us
    unnamed x17, local copies, waits for them, and re-layouts  8.19 us
    all_gather x2, waiting for transfers between devices, local(): summed = fold_rows(whole, lax.all_gather(weight, 'dp', axis=0, tiled=True))  7.91 us
    dot_general x1, matrix products, local(): pre = jnp.dot(ranges, w_ranges, preferred_element_type=jnp.float32)  6.99 us
  transfers between devices with their start and end apart: 11, of which 10 were waited for; matrix products, arithmetic and copies ran while one was open for 15% of the time, Pallas kernels for 0%

profile of v1, /device:TPU:0, one launch (start us, length us, event | category | flops | bytes accessed | tf_op | source)
XLA Modules:
  0.0 306.4 jit_solution(1768950720743668701)
XLA Ops:
  6.5 0.0 copy-start
  6.5 0.0 all-gather.9.cloned.1.call-start
  6.5 0.7 all-gather.9.cloned.1.call-update
  7.3 0.0 all-gather.5.cloned.1.call-start
  7.3 0.7 all-gather.5.cloned.1.call-update
  8.0 0.0 all-gather.7.cloned.1.call-start
  8.1 0.7 all-gather.7.cloned.1.call-update
  8.7 0.0 all-gather.11.cloned.1.call-start
  8.8 21.4 %all-gather.9.cloned.1.call-done = bf16[256,2652]{1,0:T(8,128)(2,1)} async-done(((bf16[64,2652]{1,0:T(8,128)(2,1)}), bf16[256,2652]{1,0:T(8,128)(2,1)}) %all-gather.9.cloned.1.call-update) | async-done | bytes 1357840 | tf_op jit(solution)/shard_map/all_gather | solution.py:40
  30.2 0.0 all-gather.11.cloned.1.call-update
  30.2 0.0 copy-done
  30.2 0.0 copy-start.6
  30.2 7.0 %fusion.39 = bf16[1280,512]{0,1:T(8,128)(2,1)S(1)} fusion(bf16[1280,2652]{0,1:T(8,128)(2,1)} %param.13, bf16[2652,512]{1,0:T(8,128)(2,1)S(1)} %copy-done, f32[512]{0:T(512)} %param.17, f32[512]{0:T(512)} %param.16, f32[1280]{0:T(1024)} %param.14), kind=kOutput, calls=%fused_computation.45 | convolution fusion | flops 3479306240 | bytes 10824704 | tf_op jit(solution)/shard_map/dot_general | solution.py:24
  37.2 0.0 copy-start.1
  37.2 1.0 copy-done.1
  38.3 0.2 collective-permute-start
  38.5 16.8 %collective-permute-done = bf16[1280,512]{0,1:T(8,128)(2,1)S(1)} collective-permute-done((bf16[1280,512]{0,1:T(8,128)(2,1)S(1)}, bf16[1280,512]{0,1:T(8,128)(2,1)S(1)}, u32[]{:S(2)}, u32[]{:S(2)}) %collective-permute-start) | collective-permute-done | bytes 1310752 | tf_op jit(solution)/shard_map/ppermute | solution.py:30
  55.3 0.0 copy-start.2
  55.3 1.1 copy-done.2
  56.4 0.0 collective-permute-start.1
  56.4 17.1 %collective-permute-done.1 = bf16[1280,512]{0,1:T(8,128)(2,1)} collective-permute-done((bf16[1280,512]{0,1:T(8,128)(2,1)S(1)}, bf16[1280,512]{0,1:T(8,128)(2,1)}, u32[]{:S(2)}, u32[]{:S(2)}) %collective-permute-start.1) | collective-permute-done | bytes 1310752 | tf_op jit(solution)/shard_map/ppermute | solution.py:30
  73.5 0.0 collective-permute-start.2
  73.5 0.0 copy-start.7
  73.5 7.9 %all-gather.5.cloned.1.call-done = bf16[2048,512]{1,0:T(8,128)(2,1)} async-done(((bf16[256,512]{1,0:T(8,128)(2,1)}), bf16[2048,512]{1,0:T(8,128)(2,1)}) %all-gather.5.cloned.1.call-update) | async-done | bytes 2097168 | tf_op jit(solution)/shard_map/all_gather | solution.py:37
  81.4 9.4 %collective-permute-done.2 = bf16[1280,512]{0,1:T(8,128)(2,1)} collective-permute-done((bf16[1280,512]{0,1:T(8,128)(2,1)}, bf16[1280,512]{0,1:T(8,128)(2,1)}, u32[]{:S(2)}, u32[]{:S(2)}) %collective-permute-start.2) | collective-permute-done | bytes 1310752 | tf_op jit(solution)/shard_map/ppermute | solution.py:30
  90.9 0.0 copy-done.6
  90.9 12.5 %fusion.33 = bf16[1280,512]{0,1:T(8,128)(2,1)S(1)} fusion(bf16[2048,512]{1,0:T(8,128)(2,1)} %all-gather.5.cloned.1.call-done, s32[]{:T(128)S(6)} %select_n.17, bf16[1280,512]{0,1:T(8,128)(2,1)} %collective-permute-done.2, bf16[1280,512]{0,1:T(8,128)(2,1)} %collective-permute-done.1, bf16[1280,512]{0,1:T(8,128)(2,1)} %copy-done.2, ...), kind=kOutput, calls=%fused_computation.43 | convolution fusion | flops 2728263680 | bytes 8652804 | tf_op jit(solution)/shard_map/dot_general | solution.py:12
  103.4 0.0 copy-start.3
  103.4 1.0 copy-done.3
  104.4 0.0 collective-permute-start.3
  104.4 17.0 %collective-permute-done.3 = bf16[1280,512]{0,1:T(8,128)(2,1)S(1)} collective-permute-done((bf16[1280,512]{0,1:T(8,128)(2,1)S(1)}, bf16[1280,512]{0,1:T(8,128)(2,1)S(1)}, u32[]{:S(2)}, u32[]{:S(2)}) %collective-permute-start.3) | collective-permute-done | bytes 1310752 | tf_op jit(solution)/shard_map/ppermute | solution.py:30
  121.5 0.0 copy-start.4
  121.5 1.1 copy-done.4
  122.5 0.0 collective-permute-start.4
  122.5 17.1 %collective-permute-done.4 = bf16[1280,512]{0,1:T(8,128)(2,1)} collective-permute-done((bf16[1280,512]{0,1:T(8,128)(2,1)S(1)}, bf16[1280,512]{0,1:T(8,128)(2,1)}, u32[]{:S(2)}, u32[]{:S(2)}) %collective-permute-start.4) | collective-permute-done | bytes 1310752 | tf_op jit(solution)/shard_map/ppermute | solution.py:30
  139.6 0.0 collective-permute-start.5
  139.7 0.0 all-gather.7.cloned.1.call-done
  139.7 17.3 %collective-permute-done.5 = bf16[1280,512]{0,1:T(8,128)(2,1)} collective-permute-done((bf16[1280,512]{0,1:T(8,128)(2,1)}, bf16[1280,512]{0,1:T(8,128)(2,1)}, u32[]{:S(2)}, u32[]{:S(2)}) %collective-permute-start.5) | collective-permute-done | bytes 1310752 | tf_op jit(solution)/shard_map/ppermute | solution.py:30
  157.0 0.0 copy-done.7
  157.0 13.4 %fusion.36 = bf16[1280,512]{0,1:T(8,128)(2,1)} fusion(bf16[2048,512]{1,0:T(8,128)(2,1)} %all-gather.7.cloned.1.call-done, s32[]{:T(128)S(6)} %select_n.17, bf16[1280,512]{0,1:T(8,128)(2,1)} %collective-permute-done.5, bf16[1280,512]{0,1:T(8,128)(2,1)} %collective-permute-done.4, bf16[1280,512]{0,1:T(8,128)(2,1)} %copy-done.4, ...), kind=kOutput, calls=%fused_computation.44 | convolution fusion | flops 2728263680 | bytes 8652804 | tf_op jit(solution)/shard_map/dot_general | solution.py:12
  170.4 2.4 copy.15
  172.8 4.3 %all-to-all-start = ((bf16[4,320,512]{2,1,0:T(8,128)(2,1)}), bf16[4,320,512]{2,1,0:T(8,128)(2,1)}, u32[]{:S(2)}, u32[]{:S(2)}) async-start(bf16[4,320,512]{2,1,0:T(8,128)(2,1)} %bitcast.10), calls=%async_computation | async-start | bytes 2621440 | tf_op jit(solution)/shard_map/all_to_all | solution.py:39
  177.1 4.2 %constant_dynamic-slice_fusion = bf16[320,2652]{0,1:T(8,128)(2,1)} fusion(bf16[1280,2652]{0,1:T(8,128)(2,1)} %param.13, s32[]{:T(128)S(6)} %select_n.13), kind=kLoop, calls=%fused_computation.49 | loop fusion | bytes 3394564 | tf_op jit(solution)/shard_map/dynamic_slice | solution.py:23
  181.3 0.0 copy-start.5
  181.3 4.0 %copy.19 = bf16[320,2652]{1,0:T(8,128)(2,1)} copy(bf16[320,2652]{0,1:T(8,128)(2,1)} %constant_dynamic-slice_fusion) | data formatting | bytes 3394560
  185.3 9.1 %all-to-all-done = bf16[4,320,512]{2,1,0:T(8,128)(2,1)} async-done(((bf16[4,320,512]{2,1,0:T(8,128)(2,1)}), bf16[4,320,512]{2,1,0:T(8,128)(2,1)}, u32[]{:S(2)}, u32[]{:S(2)}) %all-to-all-start) | async-done | bytes 1310752 | tf_op jit(solution)/shard_map/all_to_all | solution.py:39
  194.4 2.9 copy.20
  197.4 91.3 %all-gather.11.cloned.1.call-done = bf16[2048,2652]{1,0:T(8,128)(2,1)} async-done(((bf16[256,2652]{1,0:T(8,128)(2,1)}), bf16[2048,2652]{1,0:T(8,128)(2,1)}) %all-gather.11.cloned.1.call-update) | async-done | bytes 10862608 | tf_op jit(solution)/shard_map/all_gather | solution.py:42
  288.7 0.0 copy-done.5
  288.7 9.1 %convert_reduce_fusion = (f32[320]{0:T(512)S(1)}, f32[320]{0:T(512)S(1)}, f32[320,2652]{1,0:T(8,128)S(1)}) fusion(bf16[320,2652]{1,0:T(8,128)(2,1)} %copy.19, f32[2652]{0:T(1024)S(1)} %copy-done.5, bf16[320,2048]{1,0:T(8,128)(2,1)} %bitcast.11, bf16[2048,2652]{1,0:T(8,128)(2,1)} %all-gather.11.cloned.1.call-done), kind=kOutput, calls=%fused_computation.32 | convolution fusion | flops 3480272128 | bytes 17278320 | tf_op jit(solution)/shard_map/dot_general | solution.py:12
  297.8 2.1 broadcast_subtract_fusion
  (1 shorter events, 0.0 us)
Async XLA Ops:
  6.5 23.7 %copy-start = (bf16[2652,512]{1,0:T(8,128)(2,1)S(1)}, bf16[2652,512]{1,0:T(8,128)(2,1)}, u32[]{:S(2)}) copy-start(bf16[2652,512]{1,0:T(8,128)(2,1)} %param.15) | copy-start | bytes 8146948
  6.5 23.6 %all-gather.9.cloned.1.call-start = ((), (), s32[]{:S(2)}) async-start(), calls=%async_computation.3 | async-start | bytes 1720320 | tf_op jit(solution)/shard_map/all_gather | solution.py:40
  7.3 74.2 %all-gather.5.cloned.1.call-start = ((), (), s32[]{:S(2)}) async-start(), calls=%async_computation.1 | async-start | bytes 2359296 | tf_op jit(solution)/shard_map/all_gather | solution.py:37
  8.0 131.6 %all-gather.7.cloned.1.call-start = ((), (), s32[]{:S(2)}) async-start(), calls=%async_computation.2 | async-start | bytes 2359296 | tf_op jit(solution)/shard_map/all_gather | solution.py:37
  8.7 280.0 %all-gather.11.cloned.1.call-start = ((), (), s32[]{:S(2)}) async-start(), calls=%async_computation.4 | async-start | bytes 12386304 | tf_op jit(solution)/shard_map/all_gather | solution.py:42
  30.2 60.6 %copy-start.6 = (f32[512]{0:T(512)S(1)}, f32[512]{0:T(512)}, u32[]{:S(2)}) copy-start(f32[512]{0:T(512)} %param.19) | copy-start | bytes 6148
  37.2 1.1 copy-start.1
  38.3 17.0 %collective-permute-start = (bf16[1280,512]{0,1:T(8,128)(2,1)S(1)}, bf16[1280,512]{0,1:T(8,128)(2,1)S(1)}, u32[]{:S(2)}, u32[]{:S(2)}) collective-permute-start(bf16[1280,512]{0,1:T(8,128)(2,1)S(1)} %fusion.39), channel_id=1, source_target_pairs={{0,1},{1,2},{2,3},{3,0},{4,5},{5,6},{6,7},{7,4},{8,9},{9,10},{10,1... | collective-permute-start | bytes 3932168 | tf_op jit(solution)/shard_map/ppermute | solution.py:30
  55.3 1.1 copy-start.2
  56.4 17.1 %collective-permute-start.1 = (bf16[1280,512]{0,1:T(8,128)(2,1)S(1)}, bf16[1280,512]{0,1:T(8,128)(2,1)}, u32[]{:S(2)}, u32[]{:S(2)}) collective-permute-start(bf16[1280,512]{0,1:T(8,128)(2,1)S(1)} %collective-permute-done), channel_id=1, source_target_pairs={{0,1},{1,2},{2,3},{3,0},{4,5},{5,6},{6,7},{7,4},{8,9},{9,10},{10,1... | collective-permute-start | bytes 3932168 | tf_op jit(solution)/shard_map/ppermute | solution.py:30
  73.5 17.3 %collective-permute-start.2 = (bf16[1280,512]{0,1:T(8,128)(2,1)}, bf16[1280,512]{0,1:T(8,128)(2,1)}, u32[]{:S(2)}, u32[]{:S(2)}) collective-permute-start(bf16[1280,512]{0,1:T(8,128)(2,1)} %collective-permute-done.1), channel_id=1, source_target_pairs={{0,1},{1,2},{2,3},{3,0},{4,5},{5,6},{6,7},{7,4},{8,9},{9,10},{10,1... | collective-permute-start | bytes 3932168 | tf_op jit(solution)/shard_map/ppermute | solution.py:30
  73.5 83.5 %copy-start.7 = (f32[512]{0:T(512)S(1)}, f32[512]{0:T(512)}, u32[]{:S(2)}) copy-start(f32[512]{0:T(512)} %param.21) | copy-start | bytes 6148
  103.4 1.1 copy-start.3
  104.4 17.0 %collective-permute-start.3 = (bf16[1280,512]{0,1:T(8,128)(2,1)S(1)}, bf16[1280,512]{0,1:T(8,128)(2,1)S(1)}, u32[]{:S(2)}, u32[]{:S(2)}) collective-permute-start(bf16[1280,512]{0,1:T(8,128)(2,1)S(1)} %fusion.33), channel_id=1, source_target_pairs={{0,1},{1,2},{2,3},{3,0},{4,5},{5,6},{6,7},{7,4},{8,9},{9,10},{10,1... | collective-permute-start | bytes 3932168 | tf_op jit(solution)/shard_map/ppermute | solution.py:30
  121.5 1.1 copy-start.4
  122.5 17.1 %collective-permute-start.4 = (bf16[1280,512]{0,1:T(8,128)(2,1)S(1)}, bf16[1280,512]{0,1:T(8,128)(2,1)}, u32[]{:S(2)}, u32[]{:S(2)}) collective-permute-start(bf16[1280,512]{0,1:T(8,128)(2,1)S(1)} %collective-permute-done.3), channel_id=1, source_target_pairs={{0,1},{1,2},{2,3},{3,0},{4,5},{5,6},{6,7},{7,4},{8,9},{9,10},{10,1... | collective-permute-start | bytes 3932168 | tf_op jit(solution)/shard_map/ppermute | solution.py:30
  139.6 17.3 %collective-permute-start.5 = (bf16[1280,512]{0,1:T(8,128)(2,1)}, bf16[1280,512]{0,1:T(8,128)(2,1)}, u32[]{:S(2)}, u32[]{:S(2)}) collective-permute-start(bf16[1280,512]{0,1:T(8,128)(2,1)} %collective-permute-done.4), channel_id=1, source_target_pairs={{0,1},{1,2},{2,3},{3,0},{4,5},{5,6},{6,7},{7,4},{8,9},{9,10},{10,1... | collective-permute-start | bytes 3932168 | tf_op jit(solution)/shard_map/ppermute | solution.py:30
  172.8 21.6 %all-to-all-start = ((bf16[4,320,512]{2,1,0:T(8,128)(2,1)}), bf16[4,320,512]{2,1,0:T(8,128)(2,1)}, u32[]{:S(2)}, u32[]{:S(2)}) async-start(bf16[4,320,512]{2,1,0:T(8,128)(2,1)} %bitcast.10), calls=%async_computation | async-start | bytes 2621440 | tf_op jit(solution)/shard_map/all_to_all | solution.py:39
  181.3 107.4 %copy-start.5 = (f32[2652]{0:T(1024)S(1)}, f32[2652]{0:T(1024)}, u32[]{:S(2)}) copy-start(f32[2652]{0:T(1024)} %param.23) | copy-start | bytes 31828
Sparse Core Ops, SparseCore 0:
  8.9 21.2 all-gather.8
  32.3 49.0 all-gather.4
  83.6 47.6 all-gather.6
  133.2 155.4 all-gather.10
